TPU v7x, 32 devices: a whole 2x2x4 slice. The times are simulated.
32 devices in a mesh: dp: 8 (over z, x), mp: 4 (over y, core).
Axes of the slice: x: 2, y: 2, z: 4, core: 2. Of those that a mesh axis runs over, the one named last changes fastest.
Arguments:
- hidden_in: bfloat16 [8192, 2048], P('dp', 'mp'), may hold values from -6 to 6
- token_ids: int32 [8192], P('dp'), may hold values from 0 to 128001, as said below
- passage_counts: int32 [16], P('dp'), may hold values from 1 to 4, as said below
- positive_doc: int32 [1024], P('dp'), may hold values from 0 to 15
- queries: bfloat16 [1024, 2048], P('dp', 'mp'), may hold values from -6 to 6
- norm_gain: float32 [2048], replicated, may hold values from 0.5 to 1.5
- w_gate: bfloat16 [2048, 7168], P(None, 'mp'), may hold values from -0.125 to 0.125
- w_up: bfloat16 [2048, 7168], P(None, 'mp'), may hold values from -0.125 to 0.125
- w_down: bfloat16 [7168, 2048], P('mp'), may hold values from -0.0625 to 0.0625
Outputs:
- query_loss: float32 [1024], P('dp')
- hidden_grad: bfloat16 [8192, 2048], P('dp', 'mp')
Inputs may be any that keep to these rules, and one draw needn't show every extreme that they name: `passage_counts`: A document has 1 to 4 passages; every draw has a dp index whose documents all have 4. The live passages hold 40 passages in all. `token_ids`: 128001 marks padding; it stands only at the tail of a document's last live passage, and every live passage has a token that is not padding.
All inputs are finite; a program needn't handle non-finite values.
Results may differ from a plain program's by a relative error of at most 0.023.
Values may be sent and summed in bfloat16 or wider, within the bound.
A program may use at most 128 MiB of HBM per device.

v0:
```python
import jax
import jax.numpy as jnp
from jax import lax
from jax.sharding import PartitionSpec as P

L = 128
pad_token = 128001
score_scale = 20.0
loss_seed = 4096.0
norm_epsilon = 1e-05
unit_epsilon = 1e-06


def contract_rows(left, right):
    return lax.dot_general(
        left, right, (((1,), (1,)), ((), ())), preferred_element_type=jnp.float32
    )


def packing_order(received_flag, received_mask, slot_capacity):
    flag = received_flag.reshape(-1).astype(jnp.float32)
    place = jnp.cumsum(flag) - flag
    packed_rows = flag[None, :] * (
        place[None, :] == jnp.arange(slot_capacity, dtype=jnp.float32)[:, None]
    ).astype(jnp.float32)
    packed_half_rows = packed_rows.astype(jnp.bfloat16)
    task_row_mask = jnp.dot(
        packed_half_rows,
        received_mask.reshape(flag.shape[0], -1),
        preferred_element_type=jnp.float32,
    )
    return (packed_rows, packed_half_rows, task_row_mask)


def per_device(
    hidden_in, token_ids, passage_counts, positive_doc, queries, norm_gain, w_gate, w_up, w_down
):
    dp_count = lax.axis_size("dp")
    row_count, part_width = hidden_in.shape
    model_width = norm_gain.shape[0]
    docs_here = passage_counts.shape[0]
    quarters = 4
    block_len = L // quarters
    src_blocks = row_count // block_len
    most_pass = src_blocks // (docs_here * quarters)
    slot_count = src_blocks // dp_count
    slot_capacity = docs_here * 2 * (most_pass + 1)
    passes_here = docs_here * most_pass
    received = dp_count * slot_count
    all_counts = lax.all_gather(passage_counts, "dp", axis=0, tiled=True)
    doc_total = all_counts.shape[0]
    before = (jnp.arange(doc_total, dtype=jnp.int32) < lax.axis_index("dp") * docs_here).astype(
        jnp.int32
    )
    offset = quarters * jnp.sum(all_counts * before)
    block_index = jnp.arange(src_blocks, dtype=jnp.int32)
    live_block = block_index // quarters % most_pass < jnp.repeat(
        passage_counts, most_pass * quarters
    )
    live_int = live_block.astype(jnp.int32)
    global_order = offset + jnp.cumsum(live_int) - live_int
    target = global_order % dp_count
    token_live = (token_ids.reshape(src_blocks, block_len) != pad_token) & live_block[:, None]
    device_hit = live_block.astype(jnp.float32)[:, None] * (
        target[:, None] == jnp.arange(dp_count, dtype=jnp.int32)[None, :]
    ).astype(jnp.float32)
    earlier = jnp.cumsum(device_hit, axis=0) - device_hit
    slot_match = (
        earlier[:, :, None] == jnp.arange(slot_count, dtype=jnp.float32)[None, None, :]
    ).astype(jnp.float32)
    select = (device_hit[:, :, None] * slot_match).reshape(src_blocks, received).T
    select_half = select.astype(jnp.bfloat16)
    send_mask = jnp.dot(
        select_half, token_live.astype(jnp.bfloat16), preferred_element_type=jnp.float32
    )
    send_mask = send_mask.astype(jnp.bfloat16).reshape(dp_count, slot_count, block_len)
    send_flag = jnp.sum(select, axis=1).astype(jnp.bfloat16).reshape(dp_count, slot_count)
    mp_start = lax.axis_index("mp") * part_width
    send = jnp.dot(
        select_half,
        hidden_in.reshape(src_blocks, block_len * part_width),
        preferred_element_type=jnp.float32,
    )
    send = send.astype(jnp.bfloat16).reshape(dp_count, slot_count, block_len, part_width)
    got, received_mask, received_flag = (
        lax.all_to_all(send, "dp", split_axis=0, concat_axis=0, tiled=True),
        lax.all_to_all(send_mask, "dp", split_axis=0, concat_axis=0, tiled=True),
        lax.all_to_all(send_flag, "dp", split_axis=0, concat_axis=0, tiled=True),
    )
    packed_rows, packed_half_rows, task_row_mask = packing_order(
        received_flag, received_mask, slot_capacity
    )
    own_rows = jnp.dot(
        packed_half_rows,
        got.reshape(received, block_len * part_width),
        preferred_element_type=jnp.float32,
    )
    own_rows = own_rows.astype(jnp.bfloat16).reshape(slot_capacity * block_len, part_width)
    task_rows = lax.all_gather(own_rows, "mp", axis=1, tiled=True)
    row_float = task_rows.astype(jnp.float32)
    rms_scale = lax.rsqrt(jnp.mean(row_float * row_float, axis=1, keepdims=True) + norm_epsilon)
    normed = (row_float * rms_scale * norm_gain[None, :]).astype(jnp.bfloat16)
    gate = jnp.dot(normed, w_gate, preferred_element_type=jnp.float32)
    up = jnp.dot(normed, w_up, preferred_element_type=jnp.float32)
    sigmoid_gate = jax.nn.sigmoid(gate)
    hidden = (gate * sigmoid_gate * up).astype(jnp.bfloat16)
    layer_part = jnp.dot(hidden, w_down, preferred_element_type=jnp.float32)
    token_weight = task_row_mask[:, :, None]
    layer_pool = jnp.sum(
        layer_part.reshape(slot_capacity, block_len, model_width) * token_weight, axis=1
    )
    layer_pool = lax.psum_scatter(
        layer_pool.astype(jnp.bfloat16), "mp", scatter_dimension=1, tiled=True
    ).astype(jnp.float32)
    own_input = own_rows.astype(jnp.float32)
    pooled = (
        jnp.sum(own_input.reshape(slot_capacity, block_len, part_width) * token_weight, axis=1)
        + layer_pool
    )
    spread = jnp.dot(packed_rows.T, pooled, precision=lax.Precision.HIGHEST)
    home = lax.all_to_all(
        spread.reshape(dp_count, slot_count, part_width).astype(jnp.bfloat16),
        "dp",
        split_axis=0,
        concat_axis=0,
        tiled=True,
    ).astype(jnp.float32)
    block_sums = jnp.dot(
        select.T, home.reshape(received, part_width), precision=lax.Precision.HIGHEST
    )
    passage_sum = block_sums.reshape(passes_here, quarters, part_width).sum(axis=1)
    token_total = jnp.sum(
        token_live.reshape(passes_here, quarters * block_len).astype(jnp.float32), axis=1
    )
    divisor = jnp.maximum(token_total, 1.0)
    passage_vec = (passage_sum / divisor[:, None]).astype(jnp.bfloat16)
    all_vec = lax.all_gather(passage_vec, "dp", axis=0, tiled=True)
    pass_total = all_vec.shape[0]
    all_live = (
        jnp.arange(pass_total, dtype=jnp.int32) % most_pass < jnp.repeat(all_counts, most_pass)
    ).astype(jnp.float32)
    vec_float = all_vec.astype(jnp.float32)
    query_float = queries.astype(jnp.float32)
    score_part = contract_rows(queries, all_vec)
    raw_score, passage_sq, query_sq = (
        lax.psum(score_part.astype(jnp.bfloat16), "mp").astype(jnp.float32),
        lax.psum(jnp.sum(vec_float * vec_float, axis=1).astype(jnp.bfloat16), "mp").astype(
            jnp.float32
        ),
        lax.psum(jnp.sum(query_float * query_float, axis=1).astype(jnp.bfloat16), "mp").astype(
            jnp.float32
        ),
    )
    query_scale = lax.rsqrt(query_sq + unit_epsilon)
    passage_scale = lax.rsqrt(passage_sq + unit_epsilon)
    scores = score_scale * raw_score * query_scale[:, None] * passage_scale[None, :]
    weights = all_live[None, :] * jnp.exp(scores)
    doc_mass = weights.reshape(queries.shape[0], doc_total, most_pass).sum(axis=2)
    total_mass = doc_mass.sum(axis=1)
    positive_hit = (
        positive_doc[:, None] == jnp.arange(doc_total, dtype=jnp.int32)[None, :]
    ).astype(jnp.float32)
    positive_mass = jnp.sum(doc_mass * positive_hit, axis=1)
    query_loss = jnp.log(total_mass) - jnp.log(positive_mass)
    positive_pass = jnp.repeat(positive_hit, most_pass, axis=1)
    coefficient = (
        loss_seed
        * score_scale
        * query_scale[:, None]
        * (weights / total_mass[:, None] - positive_pass * weights / positive_mass[:, None])
    )
    weighted_queries = lax.dot_general(
        coefficient.astype(jnp.bfloat16),
        queries,
        (((0,), (0,)), ((), ())),
        preferred_element_type=jnp.float32,
    )
    norm_term = jnp.sum(coefficient * raw_score, axis=0)
    vec_grad, norm_grad = (
        lax.psum_scatter(
            weighted_queries.astype(jnp.bfloat16), "dp", scatter_dimension=0, tiled=True
        ).astype(jnp.float32),
        lax.psum_scatter(
            norm_term.astype(jnp.bfloat16), "dp", scatter_dimension=0, tiled=True
        ).astype(jnp.float32),
    )
    own_scale = lax.dynamic_slice_in_dim(
        passage_scale, lax.axis_index("dp") * passes_here, passes_here
    )
    own_vec = passage_vec.astype(jnp.float32)
    vec_change = own_scale[:, None] * vec_grad - own_vec * (own_scale**3 * norm_grad)[:, None]
    token_grad = (vec_change / divisor[:, None]).astype(jnp.bfloat16)
    block_grad = jnp.repeat(token_grad, quarters, axis=0)
    grad_send = jnp.dot(select_half, block_grad, preferred_element_type=jnp.float32).astype(
        jnp.bfloat16
    )
    grad_got = lax.all_to_all(
        grad_send.reshape(dp_count, slot_count, part_width),
        "dp",
        split_axis=0,
        concat_axis=0,
        tiled=True,
    )
    grad_task = jnp.dot(
        packed_half_rows, grad_got.reshape(received, part_width), preferred_element_type=jnp.float32
    ).astype(jnp.bfloat16)
    grad_full = lax.all_gather(grad_task, "mp", axis=1, tiled=True)
    out_grad = (
        (token_weight * grad_full[:, None, :].astype(jnp.float32))
        .astype(jnp.bfloat16)
        .reshape(slot_capacity * block_len, model_width)
    )
    own_out_grad = (token_weight * grad_task[:, None, :].astype(jnp.float32)).reshape(
        slot_capacity * block_len, part_width
    )
    hidden_grad = contract_rows(out_grad, w_down)
    gate_grad = (hidden_grad * up * sigmoid_gate * (1.0 + gate * (1.0 - sigmoid_gate))).astype(
        jnp.bfloat16
    )
    up_grad = (hidden_grad * gate * sigmoid_gate).astype(jnp.bfloat16)
    normed_grad = contract_rows(gate_grad, w_gate) + contract_rows(up_grad, w_up)
    own_gain = lax.dynamic_slice_in_dim(norm_gain, mp_start, part_width)
    normed_full = lax.psum(normed_grad.astype(jnp.bfloat16), "mp").astype(jnp.float32)
    inner = jnp.mean(row_float * norm_gain[None, :] * normed_full, axis=1)
    own_normed = lax.dynamic_slice_in_dim(normed_full, mp_start, part_width, 1)
    input_grad = (
        own_out_grad
        + rms_scale * own_gain[None, :] * own_normed
        - own_input * rms_scale**3 * inner[:, None]
    )
    input_half = input_grad.astype(jnp.bfloat16).reshape(slot_capacity, block_len * part_width)
    back = jnp.dot(packed_half_rows.T, input_half, preferred_element_type=jnp.float32).astype(
        jnp.bfloat16
    )
    back_got = lax.all_to_all(
        back.reshape(dp_count, slot_count, block_len * part_width),
        "dp",
        split_axis=0,
        concat_axis=0,
        tiled=True,
    )
    grad_rows = jnp.dot(
        select_half.T,
        back_got.reshape(received, block_len * part_width),
        preferred_element_type=jnp.float32,
    )
    return (query_loss, grad_rows.astype(jnp.bfloat16).reshape(row_count, part_width))


def solution(mesh):
    return jax.shard_map(
        per_device,
        mesh=mesh,
        in_specs=(
            P("dp", "mp"),
            P("dp"),
            P("dp"),
            P("dp"),
            P("dp", "mp"),
            P(),
            P(None, "mp"),
            P(None, "mp"),
            P("mp", None),
        ),
        out_specs=(P("dp"), P("dp", "mp")),
        check_vma=False,
    )
```

profile of v0, /device:TPU:0, one launch (start us, length us, event | category | flops | bytes accessed | tf_op | source)
XLA Modules:
  0.0 407.2 jit_solution(3093660262261133668)
XLA Ops:
  11.1 13.1 %all-reduce = s32[16]{0:T(128)S(1)} all-reduce(s32[16]{0:T(128)S(1)} %dynamic-update-slice), channel_id=1, replica_groups=mesh['dp'=8,'mp'=4] {'dp'}, use_global_device_ids=true, to_apply=%add | all-reduce | flops 16 | bytes 128
  26.8 3.3 all-to-all-start
  33.7 3.0 all-to-all-done
  36.6 3.7 all-to-all-start.1
  40.7 21.8 %all-to-all-done.1 = bf16[8,4,32,512]{3,2,1,0:T(8,128)(2,1)S(1)} async-done(((bf16[8,4,32,512]{3,2,1,0:T(8,128)(2,1)}), bf16[8,4,32,512]{3,2,1,0:T(8,128)(2,1)S(1)}, u32[]{:S(2)}, u32[]{:S(2)}) %all-to-all-start.1) | async-done | bytes 1048608 | tf_op jit(solution)/shard_map/all_to_all | solution.py:86
  65.8 3.4 all-to-all-start.2
  70.1 5.6 %all-to-all-done.2 = bf16[8,4,32]{2,1,0:T(4,128)(2,1)S(1)} async-done(((bf16[8,4,32]{2,1,0:T(4,128)(2,1)}), bf16[8,4,32]{2,1,0:T(4,128)(2,1)S(1)}, u32[]{:S(2)}, u32[]{:S(2)}) %all-to-all-start.2) | async-done | bytes 2080 | tf_op jit(solution)/shard_map/all_to_all | solution.py:87
  75.8 2.1 copy.62
  77.9 11.5 %all-gather.2.cloned.1.call-done = bf16[640,2048]{1,0:T(8,128)(2,1)} async-done(((bf16[640,512]{1,0:T(8,128)(2,1)}), bf16[640,2048]{1,0:T(8,128)(2,1)}) %all-gather.2.cloned.1.call-update) | async-done | bytes 2621456 | tf_op jit(solution)/shard_map/all_gather | solution.py:99
  89.4 2.5 fusion
  92.0 9.0 %fusion.15 = f32[640,1792]{1,0:T(8,128)S(1)} fusion(bf16[2048,1792]{1,0:T(8,128)(2,1)} %param.16, bf16[640,2048]{1,0:T(8,128)(2,1)} %all-gather.2.cloned.1.call-done, f32[2048]{0:T(1024)S(1)} %copy-done.4, f32[640]{0:T(1024)S(1)} %get-tuple-element.14), kind=kOutput, calls=%fused_computation.38 | convolution fusion | flops 4702863360 | bytes 14559744 | tf_op jit(solution)/shard_map/dot_general | solution.py:104
  101.0 5.0 %fusion.17 = f32[640,1792]{1,0:T(8,128)S(1)} fusion(bf16[2048,1792]{1,0:T(8,128)(2,1)S(1)} %bitcast.76, bf16[640,2048]{1,0:T(8,128)(2,1)S(1)} %copy-done, f32[2048]{0:T(1024)S(1)} %copy-done.4, f32[640]{0:T(1024)S(1)} %get-tuple-element.14), kind=kOutput, calls=%fused_computation.39 | convolution fusion | flops 4702863360 | bytes 14559744 | tf_op jit(solution)/shard_map/dot_general | solution.py:103
  106.0 5.0 %fusion.6 = f32[640,2048]{1,0:T(8,128)S(1)} fusion(bf16[1792,2048]{1,0:T(8,128)(2,1)S(1)} %bitcast.74, f32[640,1792]{1,0:T(8,128)S(1)} %fusion.15, f32[640,1792]{1,0:T(8,128)S(1)} %fusion.17), kind=kOutput, calls=%fused_computation.20 | convolution fusion | flops 4704501760 | bytes 21757952 | tf_op jit(solution)/shard_map/dot_general | solution.py:107
  111.1 1.6 multiply_reduce_fusion
  112.7 1.6 fusion.10
  114.3 18.1 %reduce-scatter.3.cloned.1.call-done = bf16[20,512]{1,0:T(8,128)(2,1)} async-done(((bf16[20,2048]{1,0:T(8,128)(2,1)}), bf16[20,512]{1,0:T(8,128)(2,1)}) %reduce-scatter.3.cloned.1.call-update) | async-done | bytes 20496 | tf_op jit(solution)/shard_map/reduce_scatter | solution.py:112
  134.0 5.5 %all-to-all-start.3 = ((bf16[8,4,512]{2,1,0:T(4,128)(2,1)}), bf16[8,4,512]{2,1,0:T(4,128)(2,1)S(1)}, u32[]{:S(2)}, u32[]{:S(2)}) async-start(bf16[8,4,512]{2,1,0:T(4,128)(2,1)} %convert_element_type.242), calls=%async_computation.4 | async-start | bytes 65536 | tf_op jit(solution)/shard_map/all_to_all | solution.py:121
  140.6 5.6 %all-to-all-done.3 = bf16[8,4,512]{2,1,0:T(4,128)(2,1)S(1)} async-done(((bf16[8,4,512]{2,1,0:T(4,128)(2,1)}), bf16[8,4,512]{2,1,0:T(4,128)(2,1)S(1)}, u32[]{:S(2)}, u32[]{:S(2)}) %all-to-all-start.3) | async-done | bytes 32800 | tf_op jit(solution)/shard_map/all_to_all | solution.py:121
  146.5 30.6 %all_gather.14 = bf16[64,512]{1,0:T(8,128)(2,1)S(1)} all-gather(bf16[8,512]{1,0:T(8,128)(2,1)S(1)} %divide_convert_fusion.1), channel_id=1, replica_groups=mesh['dp'=8,'mp'=4] {'dp'}, dimensions={0}, use_global_device_ids=true | all-gather | bytes 73728 | tf_op jit(solution)/shard_map/all_gather | solution.py:137
  177.3 10.4 %all-reduce.2 = (bf16[128,64]{0,1:T(8,128)(2,1)S(1)}, bf16[64]{0:T(256)(128)(2,1)S(1)}, bf16[128]{0:T(256)(128)(2,1)S(1)}) all-reduce(bf16[128,64]{0,1:T(8,128)(2,1)S(1)} %fusion.14, bf16[64]{0:T(256)(128)(2,1)S(1)} %multiply_reduce_fusion.2, bf16[128]{0:T(256)(128)(2,1)S(1)} %multiply_reduce_fusion.1), channel_id=1, replica_groups=mesh['dp'=8,'mp'=4] {'mp'}, use_global_device_ids=true, to_apply=%region_11.12 | all-reduce | flops 8384 | bytes 33536 | tf_op jit(solution)/shard_map/psum | solution.py:146
  188.9 17.8 %all-reduce.1 = bf16[64]{0:T(256)(128)(2,1)S(1)} all-reduce(bf16[64]{0:T(256)(128)(2,1)S(1)} %fusion.24), channel_id=4, replica_groups=mesh['dp'=8,'mp'=4] {'dp'}, use_global_device_ids=true, to_apply=%region_21.22.clone | all-reduce | flops 64 | bytes 256
  206.8 40.9 %reduce-scatter.5.cloned.1.call-done = bf16[8,512]{1,0:T(8,128)(2,1)} async-done(((bf16[64,512]{1,0:T(8,128)(2,1)}), bf16[8,512]{1,0:T(8,128)(2,1)}) %reduce-scatter.5.cloned.1.call-update) | async-done | bytes 8208 | tf_op jit(solution)/shard_map/reduce_scatter | solution.py:180
  249.3 3.6 all-to-all-start.4
  253.1 6.6 %all-to-all-done.4 = bf16[8,4,512]{2,1,0:T(4,128)(2,1)S(1)} async-done(((bf16[8,4,512]{2,1,0:T(4,128)(2,1)}), bf16[8,4,512]{2,1,0:T(4,128)(2,1)S(1)}, u32[]{:S(2)}, u32[]{:S(2)}) %all-to-all-start.4) | async-done | bytes 32800 | tf_op jit(solution)/shard_map/all_to_all | solution.py:197
  259.8 5.5 %all_gather.15 = bf16[20,2048]{1,0:T(8,128)(2,1)S(1)} all-gather(bf16[20,512]{1,0:T(8,128)(2,1)S(1)} %get-tuple-element.22), channel_id=1, replica_groups=mesh['dp'=8,'mp'=4] {'mp'}, dimensions={1}, use_global_device_ids=true | all-gather | bytes 102400 | tf_op jit(solution)/shard_map/all_gather | solution.py:207
  265.7 9.9 %fusion.72 = f32[640,1792]{1,0:T(8,128)} fusion(bf16[640,2048]{1,0:T(8,128)(2,1)S(1)} %fusion.5, bf16[1792,2048]{1,0:T(8,128)(2,1)} %param.17), kind=kOutput, calls=%fused_computation.149 | convolution fusion | flops 4697620480 | bytes 14548992 | tf_op jit(solution)/shard_map/dot_general | solution.py:15
  275.6 14.2 %fusion.9 = f32[640,2048]{1,0:T(8,128)} fusion(bf16[2048,1792]{1,0:T(8,128)(2,1)S(1)} %bitcast.78, f32[640,1792]{1,0:T(8,128)} %copy-done.8, f32[640,1792]{1,0:T(8,128)} %fusion.72, f32[640,1792]{1,0:T(8,128)} %copy-done.9), kind=kOutput, calls=%fused_computation.23 | convolution fusion | flops 4709089280 | bytes 26345472 | tf_op jit(solution)/shard_map/dot_general | solution.py:15
  289.8 13.7 %add_convert_fusion = bf16[640,2048]{1,0:T(8,128)(2,1)} fusion(f32[640,2048]{1,0:T(8,128)} %fusion.9, bf16[2048,1792]{1,0:T(8,128)(2,1)} %param.16, f32[640,1792]{1,0:T(8,128)} %fusion.72, f32[640,1792]{1,0:T(8,128)} %copy-done.8), kind=kOutput, calls=%fused_computation.14 | convolution fusion | flops 4707123200 | bytes 24379392 | tf_op jit(solution)/shard_map/dot_general | solution.py:15
  303.6 57.3 %all-reduce.5.cloned.1.call-done = bf16[640,2048]{1,0:T(8,128)(2,1)} async-done(((bf16[640,2048]{1,0:T(8,128)(2,1)}), bf16[640,2048]{1,0:T(8,128)(2,1)}) %all-reduce.5.cloned.1.call-update) | async-done | bytes 2621456 | tf_op jit(solution)/shard_map/psum | solution.py:223
  361.0 2.8 fusion.4
  367.4 5.5 %all-to-all-start.5 = ((bf16[8,4,16384]{2,1,0:T(4,128)(2,1)}), bf16[8,4,16384]{2,1,0:T(4,128)(2,1)S(1)}, u32[]{:S(2)}, u32[]{:S(2)}) async-start(bf16[8,4,16384]{2,1,0:T(4,128)(2,1)} %reshape.491), calls=%async_computation.7 | async-start | bytes 2097152 | tf_op jit(solution)/shard_map/all_to_all | solution.py:235
  373.5 25.1 %all-to-all-done.5 = bf16[8,4,16384]{2,1,0:T(4,128)(2,1)S(1)} async-done(((bf16[8,4,16384]{2,1,0:T(4,128)(2,1)}), bf16[8,4,16384]{2,1,0:T(4,128)(2,1)S(1)}, u32[]{:S(2)}, u32[]{:S(2)}) %all-to-all-start.5) | async-done | bytes 1048608 | tf_op jit(solution)/shard_map/all_to_all | solution.py:235
  (137 shorter events, 25.6 us)
Async XLA Ops:
  26.8 9.8 %all-to-all-start = ((bf16[8,1,4]{2,1,0:T(2,128)(2,1)}), bf16[8,1,4]{2,1,0:T(2,128)(2,1)S(1)}, u32[]{:S(2)}, u32[]{:S(2)}) async-start(bf16[8,1,4]{2,1,0:T(2,128)(2,1)} %copy.53), calls=%async_computation | async-start | bytes 8192 | tf_op jit(solution)/shard_map/all_to_all | solution.py:88
  36.6 28.3 %copy-start.5 = (s32[1024]{0:T(1024)S(1)}, s32[1024]{0:T(1024)}, u32[]{:S(2)}) copy-start(s32[1024]{0:T(1024)} %param.10) | copy-start | bytes 12292
  36.6 32.9 %copy-start.7 = (s32[2]{0:T(128)S(1)}, s32[2]{0:T(128)}, u32[]{:S(2)}) copy-start(s32[2]{0:T(128)} %param.11) | copy-start | bytes 28
  36.6 33.5 %copy-start.6 = (s32[128]{0:T(128)S(1)}, s32[128]{0:T(128)}, u32[]{:S(2)}) copy-start(s32[128]{0:T(128)} %param.12) | copy-start | bytes 1540
  36.6 25.9 %all-to-all-start.1 = ((bf16[8,4,32,512]{3,2,1,0:T(8,128)(2,1)}), bf16[8,4,32,512]{3,2,1,0:T(8,128)(2,1)S(1)}, u32[]{:S(2)}, u32[]{:S(2)}) async-start(bf16[8,4,32,512]{3,2,1,0:T(8,128)(2,1)} %bitcast.17), calls=%async_computation.1 | async-start | bytes 2097152 | tf_op jit(solution)/shard_map/all_to_all | solution.py:86
  40.3 49.1 %all-gather.2.cloned.1.call-start = ((), (), s32[]{:S(2)}) async-start(), calls=%async_computation.8 | async-start | bytes 3276800 | tf_op jit(solution)/shard_map/all_gather | solution.py:99
  63.6 28.4 %copy-start.4 = (f32[2048]{0:T(1024)S(1)}, f32[2048]{0:T(1024)}, u32[]{:S(2)}) copy-start(f32[2048]{0:T(1024)} %param.14) | copy-start | bytes 24580
  65.8 9.9 %all-to-all-start.2 = ((bf16[8,4,32]{2,1,0:T(4,128)(2,1)}), bf16[8,4,32]{2,1,0:T(4,128)(2,1)S(1)}, u32[]{:S(2)}, u32[]{:S(2)}) async-start(bf16[8,4,32]{2,1,0:T(4,128)(2,1)} %bitcast.4), calls=%async_computation.2 | async-start | bytes 16384 | tf_op jit(solution)/shard_map/all_to_all | solution.py:87
  69.2 63.2 %reduce-scatter.3.cloned.1.call-start = ((), (), s32[]{:S(2)}) async-start(), calls=%async_computation.9 | async-start | bytes 122880 | tf_op jit(solution)/shard_map/reduce_scatter | solution.py:112
  89.4 11.5 %slice-start.2 = ((s8[7340032]{0:T(1024)(128)(4,1)}), s8[4194304]{0:T(1024)(128)(4,1)S(1)}, s32[]{:S(2)}) async-start(s8[7340032]{0:T(1024)(128)(4,1)} %bitcast.75), calls=%async_computation.14 | async-start | bytes 8388608
  91.9 9.0 %copy-start = (bf16[640,2048]{1,0:T(8,128)(2,1)S(1)}, bf16[640,2048]{1,0:T(8,128)(2,1)}, u32[]{:S(2)}) copy-start(bf16[640,2048]{1,0:T(8,128)(2,1)} %all-gather.2.cloned.1.call-done) | copy-start | bytes 7864324
  91.9 9.0 %slice-start.3 = ((s8[7340032]{0:T(1024)(128)(4,1)}), s8[3145728]{0:T(1024)(128)(4,1)S(1)}, s32[]{:S(2)}) async-start(s8[7340032]{0:T(1024)(128)(4,1)} %bitcast.75), calls=%async_computation.15 | async-start | bytes 6291456
  91.9 14.1 %slice-start = ((s8[7340032]{0:T(1024)(128)(4,1)}), s8[4194304]{0:T(1024)(128)(4,1)S(1)}, s32[]{:S(2)}) async-start(s8[7340032]{0:T(1024)(128)(4,1)} %bitcast.73), calls=%async_computation.12 | async-start | bytes 8388608
  101.0 5.0 %copy-start.9 = (f32[640,1792]{1,0:T(8,128)}, f32[640,1792]{1,0:T(8,128)S(1)}, u32[]{:S(2)}) copy-start(f32[640,1792]{1,0:T(8,128)S(1)} %fusion.15) | copy-start | bytes 13762564
  101.0 5.0 %slice-start.1 = ((s8[7340032]{0:T(1024)(128)(4,1)}), s8[3145728]{0:T(1024)(128)(4,1)S(1)}, s32[]{:S(2)}) async-start(s8[7340032]{0:T(1024)(128)(4,1)} %bitcast.73), calls=%async_computation.13 | async-start | bytes 6291456
  106.0 5.0 %copy-start.8 = (f32[640,1792]{1,0:T(8,128)}, f32[640,1792]{1,0:T(8,128)S(1)}, u32[]{:S(2)}) copy-start(f32[640,1792]{1,0:T(8,128)S(1)} %fusion.17) | copy-start | bytes 13762564
  111.0 28.5 %copy-start.3 = (bf16[128,512]{1,0:T(8,128)(2,1)S(1)}, bf16[128,512]{1,0:T(8,128)(2,1)}, u32[]{:S(2)}) copy-start(bf16[128,512]{1,0:T(8,128)(2,1)} %param.13) | copy-start | bytes 393220
  134.0 12.2 %all-to-all-start.3 = ((bf16[8,4,512]{2,1,0:T(4,128)(2,1)}), bf16[8,4,512]{2,1,0:T(4,128)(2,1)S(1)}, u32[]{:S(2)}, u32[]{:S(2)}) async-start(bf16[8,4,512]{2,1,0:T(4,128)(2,1)} %convert_element_type.242), calls=%async_computation.4 | async-start | bytes 65536 | tf_op jit(solution)/shard_map/all_to_all | solution.py:121
  139.5 108.2 %reduce-scatter.5.cloned.1.call-start = ((), (), s32[]{:S(2)}) async-start(), calls=%async_computation.10 | async-start | bytes 73728 | tf_op jit(solution)/shard_map/reduce_scatter | solution.py:180
  249.3 10.3 %all-to-all-start.4 = ((bf16[8,4,512]{2,1,0:T(4,128)(2,1)}), bf16[8,4,512]{2,1,0:T(4,128)(2,1)S(1)}, u32[]{:S(2)}, u32[]{:S(2)}) async-start(bf16[8,4,512]{2,1,0:T(4,128)(2,1)} %reshape.488), calls=%async_computation.6 | async-start | bytes 65536 | tf_op jit(solution)/shard_map/all_to_all | solution.py:197
  253.0 108.0 %all-reduce.5.cloned.1.call-start = ((), (), s32[]{:S(2)}) async-start(), calls=%async_computation.11 | async-start | bytes 5242880 | tf_op jit(solution)/shard_map/psum | solution.py:223
  265.4 10.2 %slice-start.4 = ((s8[7340032]{0:T(1024)(128)(4,1)}), s8[4194304]{0:T(1024)(128)(4,1)S(1)}, s32[]{:S(2)}) async-start(s8[7340032]{0:T(1024)(128)(4,1)} %bitcast.77), calls=%async_computation.16 | async-start | bytes 8388608
  265.7 9.9 %slice-start.5 = ((s8[7340032]{0:T(1024)(128)(4,1)}), s8[3145728]{0:T(1024)(128)(4,1)S(1)}, s32[]{:S(2)}) async-start(s8[7340032]{0:T(1024)(128)(4,1)} %bitcast.77), calls=%async_computation.17 | async-start | bytes 6291456
  361.0 2.9 copy-start.1
  363.8 1.1 copy-start.2
  367.4 31.1 %all-to-all-start.5 = ((bf16[8,4,16384]{2,1,0:T(4,128)(2,1)}), bf16[8,4,16384]{2,1,0:T(4,128)(2,1)S(1)}, u32[]{:S(2)}, u32[]{:S(2)}) async-start(bf16[8,4,16384]{2,1,0:T(4,128)(2,1)} %reshape.491), calls=%async_computation.7 | async-start | bytes 2097152 | tf_op jit(solution)/shard_map/all_to_all | solution.py:235
Sparse Core Ops, SparseCore 0:
  65.0 24.3 all-gather.1
  112.8 19.5 reduce-scatter.2
  188.8 58.8 reduce-scatter.4
  303.7 57.2 all-reduce.4
where the time goes:
time: 408 us; the launch traced here: 407 us
  waiting for transfers between devices  196 us (48%)
  blocking collectives  77.4 us (19%)
  matrix products  61.8 us (15%)
  starting transfers between devices  25.4 us (6%)
  local copies, waits for them, and re-layouts  16.9 us (4%)
  between operations  16.3 us (4%)
  other arithmetic  13.7 us (3%)
    psum x1, waiting for transfers between devices, per_device(): lax.psum(normed_grad.astype(jnp.bfloat16), 'mp').astype(jnp.float32)  57.3 us
    reduce_scatter x1, waiting for transfers between devices, per_device(): lax.psum_scatter(weighted_queries.astype(jnp.bfloat16), 'dp', scatter_dim...  40.9 us
    dot_general x4, matrix products, contract_rows(): lax.dot_general(left, right, (((1,), (1,)), ((), ())), preferred_element_...  37.9 us
    unnamed x2, blocking collectives  30.9 us
    all_gather x1, blocking collectives, per_device(): all_vec = lax.all_gather(passage_vec, 'dp', axis=0, tiled=True)  30.6 us
    all_to_all x1, waiting for transfers between devices, per_device(): lax.all_to_all(back.reshape(dp_count, slot_count, block_len * part_width)...  25.1 us
    all_to_all x1, waiting for transfers between devices, per_device(): lax.all_to_all(send, 'dp', split_axis=0, concat_axis=0, tiled=True)  21.8 us
    reduce_scatter x1, waiting for transfers between devices, per_device(): lax.psum_scatter(layer_pool.astype(jnp.bfloat16), 'mp', scatter_dimension...  18.1 us
  transfers between devices with their start and end apart: 10, of which 10 were waited for; matrix products, arithmetic and copies ran while one was open for 3% of the time, Pallas kernels for 0%

commit v1 on v0

--- a/solution.py
+++ b/solution.py
@@ -220,7 +220,9 @@
     up_grad = (hidden_grad * gate * sigmoid_gate).astype(jnp.bfloat16)
     normed_grad = contract_rows(gate_grad, w_gate) + contract_rows(up_grad, w_up)
     own_gain = lax.dynamic_slice_in_dim(norm_gain, mp_start, part_width)
-    normed_full = lax.psum(normed_grad.astype(jnp.bfloat16), "mp").astype(jnp.float32)
+    normed_full = jnp.sum(lax.all_gather(normed_grad.astype(jnp.bfloat16), "mp"), axis=0).astype(
+        jnp.float32
+    )
     inner = jnp.mean(row_float * norm_gain[None, :] * normed_full, axis=1)
     own_normed = lax.dynamic_slice_in_dim(normed_full, mp_start, part_width, 1)
     input_grad = (

time: 408 us -> 426 us (1.044)
  waiting for transfers between devices: 196 us -> 209 us
    all_gather x0 -> x1, waiting for transfers between devices: none -> 67.6 us  [per_device(): lax.all_gather(normed_grad.astype(jnp.bfloat16), 'mp')]
    psum x1 -> x0, waiting for transfers between devices: 57.3 us -> none  [per_device(): lax.psum(normed_grad.astype(jnp.bfloat16), 'mp').astype(jnp.float32)]
    reduce_sum x0 -> x1, other arithmetic: none -> 7.28 us  [per_device(): jnp.sum(lax.all_gather(normed_grad.astype(jnp.bfloat16), 'mp'), axis=0)]
  transfers between devices with their start and end apart: 10 -> 10, of which waited for: 10 -> 10; matrix products, arithmetic and copies ran while one was open for 3% -> 2% of each run, Pallas kernels for 0% -> 0%
where the time goes in v1:
time: 426 us; the launch traced here: 425 us
  waiting for transfers between devices  209 us (49%)
  blocking collectives  77.2 us (18%)
  matrix products  63.1 us (15%)
  starting transfers between devices  25.4 us (6%)
  other arithmetic  17.8 us (4%)
  local copies, waits for them, and re-layouts  16.6 us (4%)
  between operations  16.2 us (4%)
    all_gather x1, waiting for transfers between devices, per_device(): lax.all_gather(normed_grad.astype(jnp.bfloat16), 'mp')  67.6 us
    reduce_scatter x1, waiting for transfers between devices, per_device(): lax.psum_scatter(weighted_queries.astype(jnp.bfloat16), 'dp', scatter_dim...  41 us
    dot_general x4, matrix products, contract_rows(): lax.dot_general(left, right, (((1,), (1,)), ((), ())), preferred_element_...  38.1 us
    unnamed x2, blocking collectives  30.9 us
    all_gather x1, blocking collectives, per_device(): all_vec = lax.all_gather(passage_vec, 'dp', axis=0, tiled=True)  30.6 us
    all_to_all x1, waiting for transfers between devices, per_device(): lax.all_to_all(back.reshape(dp_count, slot_count, block_len * part_width)...  25.7 us
    all_to_all x1, waiting for transfers between devices, per_device(): lax.all_to_all(send, 'dp', split_axis=0, concat_axis=0, tiled=True)  21.8 us
    reduce_scatter x1, waiting for transfers between devices, per_device(): lax.psum_scatter(layer_pool.astype(jnp.bfloat16), 'mp', scatter_dimension...  19.5 us
  transfers between devices with their start and end apart: 10, of which 10 were waited for; matrix products, arithmetic and copies ran while one was open for 2% of the time, Pallas kernels for 0%

profile of v1, /device:TPU:0, one launch (start us, length us, event | category | flops | bytes accessed | tf_op | source)
XLA Modules:
  0.0 425.2 jit_solution(7612486885559917472)
XLA Ops:
  8.2 1.3 fusion.69
  11.1 13.1 %all-reduce = s32[16]{0:T(128)S(1)} all-reduce(s32[16]{0:T(128)S(1)} %dynamic-update-slice), channel_id=1, replica_groups=mesh['dp'=8,'mp'=4] {'dp'}, use_global_device_ids=true, to_apply=%add | all-reduce | flops 16 | bytes 128
  26.8 3.3 all-to-all-start
  30.3 1.6 reshape.477
  33.7 3.0 all-to-all-done
  36.6 3.7 all-to-all-start.1
  40.7 21.8 %all-to-all-done.1 = bf16[8,4,32,512]{3,2,1,0:T(8,128)(2,1)S(1)} async-done(((bf16[8,4,32,512]{3,2,1,0:T(8,128)(2,1)}), bf16[8,4,32,512]{3,2,1,0:T(8,128)(2,1)S(1)}, u32[]{:S(2)}, u32[]{:S(2)}) %all-to-all-start.1) | async-done | bytes 1048608 | tf_op jit(solution)/shard_map/all_to_all | solution.py:86
  65.8 3.4 all-to-all-start.2
  70.1 5.6 %all-to-all-done.2 = bf16[8,4,32]{2,1,0:T(4,128)(2,1)S(1)} async-done(((bf16[8,4,32]{2,1,0:T(4,128)(2,1)}), bf16[8,4,32]{2,1,0:T(4,128)(2,1)S(1)}, u32[]{:S(2)}, u32[]{:S(2)}) %all-to-all-start.2) | async-done | bytes 2080 | tf_op jit(solution)/shard_map/all_to_all | solution.py:87
  76.8 12.7 %all-gather.4.cloned.1.call-done = bf16[640,2048]{1,0:T(8,128)(2,1)} async-done(((bf16[640,512]{1,0:T(8,128)(2,1)}), bf16[640,2048]{1,0:T(8,128)(2,1)}) %all-gather.4.cloned.1.call-update) | async-done | bytes 2621456 | tf_op jit(solution)/shard_map/all_gather | solution.py:99
  89.4 2.5 fusion
  92.0 10.1 %fusion.15 = f32[640,1792]{1,0:T(8,128)S(1)} fusion(bf16[2048,1792]{1,0:T(8,128)(2,1)} %param.16, bf16[640,2048]{1,0:T(8,128)(2,1)} %all-gather.4.cloned.1.call-done, f32[2048]{0:T(1024)S(1)} %copy-done.4, f32[640]{0:T(1024)S(1)} %get-tuple-element.14), kind=kOutput, calls=%fused_computation.38 | convolution fusion | flops 4702863360 | bytes 14559744 | tf_op jit(solution)/shard_map/dot_general | solution.py:104
  102.1 5.0 %fusion.17 = f32[640,1792]{1,0:T(8,128)S(1)} fusion(bf16[2048,1792]{1,0:T(8,128)(2,1)S(1)} %bitcast.78, bf16[640,2048]{1,0:T(8,128)(2,1)S(1)} %copy-done, f32[2048]{0:T(1024)S(1)} %copy-done.4, f32[640]{0:T(1024)S(1)} %get-tuple-element.14), kind=kOutput, calls=%fused_computation.39 | convolution fusion | flops 4702863360 | bytes 14559744 | tf_op jit(solution)/shard_map/dot_general | solution.py:103
  107.2 5.0 %fusion.6 = f32[640,2048]{1,0:T(8,128)S(1)} fusion(bf16[1792,2048]{1,0:T(8,128)(2,1)S(1)} %bitcast.76, f32[640,1792]{1,0:T(8,128)S(1)} %fusion.15, f32[640,1792]{1,0:T(8,128)S(1)} %fusion.17), kind=kOutput, calls=%fused_computation.20 | convolution fusion | flops 4704501760 | bytes 21757952 | tf_op jit(solution)/shard_map/dot_general | solution.py:107
  112.2 1.6 multiply_reduce_fusion
  114.0 19.5 %reduce-scatter.3.cloned.1.call-done = bf16[20,512]{1,0:T(8,128)(2,1)} async-done(((bf16[20,2048]{1,0:T(8,128)(2,1)}), bf16[20,512]{1,0:T(8,128)(2,1)}) %reduce-scatter.3.cloned.1.call-update) | async-done | bytes 20496 | tf_op jit(solution)/shard_map/reduce_scatter | solution.py:112
  135.1 5.5 %all-to-all-start.3 = ((bf16[8,4,512]{2,1,0:T(4,128)(2,1)}), bf16[8,4,512]{2,1,0:T(4,128)(2,1)S(1)}, u32[]{:S(2)}, u32[]{:S(2)}) async-start(bf16[8,4,512]{2,1,0:T(4,128)(2,1)} %convert_element_type.244), calls=%async_computation.4 | async-start | bytes 65536 | tf_op jit(solution)/shard_map/all_to_all | solution.py:121
  141.7 5.6 %all-to-all-done.3 = bf16[8,4,512]{2,1,0:T(4,128)(2,1)S(1)} async-done(((bf16[8,4,512]{2,1,0:T(4,128)(2,1)}), bf16[8,4,512]{2,1,0:T(4,128)(2,1)S(1)}, u32[]{:S(2)}, u32[]{:S(2)}) %all-to-all-start.3) | async-done | bytes 32800 | tf_op jit(solution)/shard_map/all_to_all | solution.py:121
  147.6 30.6 %all_gather.20 = bf16[64,512]{1,0:T(8,128)(2,1)S(1)} all-gather(bf16[8,512]{1,0:T(8,128)(2,1)S(1)} %divide_convert_fusion.1), channel_id=1, replica_groups=mesh['dp'=8,'mp'=4] {'dp'}, dimensions={0}, use_global_device_ids=true | all-gather | bytes 73728 | tf_op jit(solution)/shard_map/all_gather | solution.py:137
  178.4 10.4 %all-reduce.2 = (bf16[128,64]{0,1:T(8,128)(2,1)S(1)}, bf16[64]{0:T(256)(128)(2,1)S(1)}, bf16[128]{0:T(256)(128)(2,1)S(1)}) all-reduce(bf16[128,64]{0,1:T(8,128)(2,1)S(1)} %fusion.14, bf16[64]{0:T(256)(128)(2,1)S(1)} %multiply_reduce_fusion.2, bf16[128]{0:T(256)(128)(2,1)S(1)} %multiply_reduce_fusion.1), channel_id=1, replica_groups=mesh['dp'=8,'mp'=4] {'mp'}, use_global_device_ids=true, to_apply=%region_11.12 | all-reduce | flops 8384 | bytes 33536 | tf_op jit(solution)/shard_map/psum | solution.py:146
  190.0 17.8 %all-reduce.1 = bf16[64]{0:T(256)(128)(2,1)S(1)} all-reduce(bf16[64]{0:T(256)(128)(2,1)S(1)} %fusion.24), channel_id=5, replica_groups=mesh['dp'=8,'mp'=4] {'dp'}, use_global_device_ids=true, to_apply=%region_21.22.clone | all-reduce | flops 64 | bytes 256
  207.9 41.0 %reduce-scatter.5.cloned.1.call-done = bf16[8,512]{1,0:T(8,128)(2,1)} async-done(((bf16[64,512]{1,0:T(8,128)(2,1)}), bf16[8,512]{1,0:T(8,128)(2,1)}) %reduce-scatter.5.cloned.1.call-update) | async-done | bytes 8208 | tf_op jit(solution)/shard_map/reduce_scatter | solution.py:180
  250.5 3.6 all-to-all-start.4
  254.2 6.6 %all-to-all-done.4 = bf16[8,4,512]{2,1,0:T(4,128)(2,1)S(1)} async-done(((bf16[8,4,512]{2,1,0:T(4,128)(2,1)}), bf16[8,4,512]{2,1,0:T(4,128)(2,1)S(1)}, u32[]{:S(2)}, u32[]{:S(2)}) %all-to-all-start.4) | async-done | bytes 32800 | tf_op jit(solution)/shard_map/all_to_all | solution.py:197
  260.9 5.3 %all_gather.21 = bf16[20,2048]{1,0:T(8,128)(2,1)S(1)} all-gather(bf16[20,512]{1,0:T(8,128)(2,1)S(1)} %get-tuple-element.22), channel_id=1, replica_groups=mesh['dp'=8,'mp'=4] {'mp'}, dimensions={1}, use_global_device_ids=true | all-gather | bytes 102400 | tf_op jit(solution)/shard_map/all_gather | solution.py:207
  266.6 9.9 %fusion.72 = f32[640,1792]{1,0:T(8,128)} fusion(bf16[640,2048]{1,0:T(8,128)(2,1)S(1)} %fusion.5, bf16[1792,2048]{1,0:T(8,128)(2,1)} %param.17), kind=kOutput, calls=%fused_computation.149 | convolution fusion | flops 4697620480 | bytes 14548992 | tf_op jit(solution)/shard_map/dot_general | solution.py:15
  276.5 14.3 %fusion.9 = f32[640,2048]{1,0:T(8,128)} fusion(bf16[2048,1792]{1,0:T(8,128)(2,1)S(1)} %bitcast.80, f32[640,1792]{1,0:T(8,128)} %copy-done.8, f32[640,1792]{1,0:T(8,128)} %fusion.72, f32[640,1792]{1,0:T(8,128)} %copy-done.9), kind=kOutput, calls=%fused_computation.23 | convolution fusion | flops 4709089280 | bytes 26345472 | tf_op jit(solution)/shard_map/dot_general | solution.py:15
  290.8 13.7 %add_convert_fusion = bf16[640,2048]{1,0:T(8,128)(2,1)} fusion(f32[640,2048]{1,0:T(8,128)} %fusion.9, bf16[2048,1792]{1,0:T(8,128)(2,1)} %param.16, f32[640,1792]{1,0:T(8,128)} %fusion.72, f32[640,1792]{1,0:T(8,128)} %copy-done.8), kind=kOutput, calls=%fused_computation.14 | convolution fusion | flops 4707123200 | bytes 24379392 | tf_op jit(solution)/shard_map/dot_general | solution.py:15
  304.7 67.6 %all-gather.6.cloned.1.call-done = bf16[2560,2048]{1,0:T(8,128)(2,1)} async-done(((bf16[640,2048]{1,0:T(8,128)(2,1)}), bf16[2560,2048]{1,0:T(8,128)(2,1)}) %all-gather.6.cloned.1.call-update) | async-done | bytes 10485776 | tf_op jit(solution)/shard_map/all_gather | solution.py:223
  372.3 7.3 %reduce_sum.151 = bf16[640,2048]{1,0:T(8,128)(2,1)S(1)} reduce(bf16[4,640,2048]{2,1,0:T(8,128)(2,1)} %bitcast.60, bf16[]{:T(256)} %constant.112.clone.1), dimensions={0}, to_apply=%region_22.23 | reduce | flops 3932160 | bytes 13107202 | tf_op jit(solution)/shard_map/reduce_sum | solution.py:223
  385.0 5.5 %all-to-all-start.5 = ((bf16[8,4,16384]{2,1,0:T(4,128)(2,1)}), bf16[8,4,16384]{2,1,0:T(4,128)(2,1)S(1)}, u32[]{:S(2)}, u32[]{:S(2)}) async-start(bf16[8,4,16384]{2,1,0:T(4,128)(2,1)} %reshape.491), calls=%async_computation.7 | async-start | bytes 2097152 | tf_op jit(solution)/shard_map/all_to_all | solution.py:237
  391.0 25.7 %all-to-all-done.5 = bf16[8,4,16384]{2,1,0:T(4,128)(2,1)S(1)} async-done(((bf16[8,4,16384]{2,1,0:T(4,128)(2,1)}), bf16[8,4,16384]{2,1,0:T(4,128)(2,1)S(1)}, u32[]{:S(2)}, u32[]{:S(2)}) %all-to-all-start.5) | async-done | bytes 1048608 | tf_op jit(solution)/shard_map/all_to_all | solution.py:237
  (138 shorter events, 25.6 us)
Async XLA Ops:
  26.8 9.8 %all-to-all-start = ((bf16[8,1,4]{2,1,0:T(2,128)(2,1)}), bf16[8,1,4]{2,1,0:T(2,128)(2,1)S(1)}, u32[]{:S(2)}, u32[]{:S(2)}) async-start(bf16[8,1,4]{2,1,0:T(2,128)(2,1)} %copy.53), calls=%async_computation | async-start | bytes 8192 | tf_op jit(solution)/shard_map/all_to_all | solution.py:88
  36.6 28.3 %copy-start.5 = (s32[1024]{0:T(1024)S(1)}, s32[1024]{0:T(1024)}, u32[]{:S(2)}) copy-start(s32[1024]{0:T(1024)} %param.10) | copy-start | bytes 12292
  36.6 32.9 %copy-start.7 = (s32[2]{0:T(128)S(1)}, s32[2]{0:T(128)}, u32[]{:S(2)}) copy-start(s32[2]{0:T(128)} %param.11) | copy-start | bytes 28
  36.6 33.5 %copy-start.6 = (s32[128]{0:T(128)S(1)}, s32[128]{0:T(128)}, u32[]{:S(2)}) copy-start(s32[128]{0:T(128)} %param.12) | copy-start | bytes 1540
  36.6 25.9 %all-to-all-start.1 = ((bf16[8,4,32,512]{3,2,1,0:T(8,128)(2,1)}), bf16[8,4,32,512]{3,2,1,0:T(8,128)(2,1)S(1)}, u32[]{:S(2)}, u32[]{:S(2)}) async-start(bf16[8,4,32,512]{3,2,1,0:T(8,128)(2,1)} %bitcast.18), calls=%async_computation.1 | async-start | bytes 2097152 | tf_op jit(solution)/shard_map/all_to_all | solution.py:86
  40.3 49.1 %all-gather.4.cloned.1.call-start = ((), (), s32[]{:S(2)}) async-start(), calls=%async_computation.8 | async-start | bytes 3276800 | tf_op jit(solution)/shard_map/all_gather | solution.py:99
  63.6 28.4 %copy-start.4 = (f32[2048]{0:T(1024)S(1)}, f32[2048]{0:T(1024)}, u32[]{:S(2)}) copy-start(f32[2048]{0:T(1024)} %param.14) | copy-start | bytes 24580
  65.8 9.9 %all-to-all-start.2 = ((bf16[8,4,32]{2,1,0:T(4,128)(2,1)}), bf16[8,4,32]{2,1,0:T(4,128)(2,1)S(1)}, u32[]{:S(2)}, u32[]{:S(2)}) async-start(bf16[8,4,32]{2,1,0:T(4,128)(2,1)} %bitcast.4), calls=%async_computation.2 | async-start | bytes 16384 | tf_op jit(solution)/shard_map/all_to_all | solution.py:87
  69.2 64.3 %reduce-scatter.3.cloned.1.call-start = ((), (), s32[]{:S(2)}) async-start(), calls=%async_computation.9 | async-start | bytes 122880 | tf_op jit(solution)/shard_map/reduce_scatter | solution.py:112
  89.4 12.7 %slice-start.2 = ((s8[7340032]{0:T(1024)(128)(4,1)}), s8[4194304]{0:T(1024)(128)(4,1)S(1)}, s32[]{:S(2)}) async-start(s8[7340032]{0:T(1024)(128)(4,1)} %bitcast.77), calls=%async_computation.14 | async-start | bytes 8388608
  89.4 17.7 %slice-start = ((s8[7340032]{0:T(1024)(128)(4,1)}), s8[4194304]{0:T(1024)(128)(4,1)S(1)}, s32[]{:S(2)}) async-start(s8[7340032]{0:T(1024)(128)(4,1)} %bitcast.75), calls=%async_computation.12 | async-start | bytes 8388608
  91.9 10.2 %copy-start = (bf16[640,2048]{1,0:T(8,128)(2,1)S(1)}, bf16[640,2048]{1,0:T(8,128)(2,1)}, u32[]{:S(2)}) copy-start(bf16[640,2048]{1,0:T(8,128)(2,1)} %all-gather.4.cloned.1.call-done) | copy-start | bytes 7864324
  91.9 10.2 %slice-start.3 = ((s8[7340032]{0:T(1024)(128)(4,1)}), s8[3145728]{0:T(1024)(128)(4,1)S(1)}, s32[]{:S(2)}) async-start(s8[7340032]{0:T(1024)(128)(4,1)} %bitcast.77), calls=%async_computation.15 | async-start | bytes 6291456
  91.9 15.2 %slice-start.1 = ((s8[7340032]{0:T(1024)(128)(4,1)}), s8[3145728]{0:T(1024)(128)(4,1)S(1)}, s32[]{:S(2)}) async-start(s8[7340032]{0:T(1024)(128)(4,1)} %bitcast.75), calls=%async_computation.13 | async-start | bytes 6291456
  102.1 5.0 %copy-start.9 = (f32[640,1792]{1,0:T(8,128)}, f32[640,1792]{1,0:T(8,128)S(1)}, u32[]{:S(2)}) copy-start(f32[640,1792]{1,0:T(8,128)S(1)} %fusion.15) | copy-start | bytes 13762564
  107.1 5.0 %copy-start.8 = (f32[640,1792]{1,0:T(8,128)}, f32[640,1792]{1,0:T(8,128)S(1)}, u32[]{:S(2)}) copy-start(f32[640,1792]{1,0:T(8,128)S(1)} %fusion.17) | copy-start | bytes 13762564
  112.2 28.5 %copy-start.3 = (bf16[128,512]{1,0:T(8,128)(2,1)S(1)}, bf16[128,512]{1,0:T(8,128)(2,1)}, u32[]{:S(2)}) copy-start(bf16[128,512]{1,0:T(8,128)(2,1)} %param.13) | copy-start | bytes 393220
  135.1 12.2 %all-to-all-start.3 = ((bf16[8,4,512]{2,1,0:T(4,128)(2,1)}), bf16[8,4,512]{2,1,0:T(4,128)(2,1)S(1)}, u32[]{:S(2)}, u32[]{:S(2)}) async-start(bf16[8,4,512]{2,1,0:T(4,128)(2,1)} %convert_element_type.244), calls=%async_computation.4 | async-start | bytes 65536 | tf_op jit(solution)/shard_map/all_to_all | solution.py:121
  140.6 108.3 %reduce-scatter.5.cloned.1.call-start = ((), (), s32[]{:S(2)}) async-start(), calls=%async_computation.10 | async-start | bytes 73728 | tf_op jit(solution)/shard_map/reduce_scatter | solution.py:180
  250.5 10.3 %all-to-all-start.4 = ((bf16[8,4,512]{2,1,0:T(4,128)(2,1)}), bf16[8,4,512]{2,1,0:T(4,128)(2,1)S(1)}, u32[]{:S(2)}, u32[]{:S(2)}) async-start(bf16[8,4,512]{2,1,0:T(4,128)(2,1)} %reshape.488), calls=%async_computation.6 | async-start | bytes 65536 | tf_op jit(solution)/shard_map/all_to_all | solution.py:197
  254.1 118.2 %all-gather.6.cloned.1.call-start = ((), (), s32[]{:S(2)}) async-start(), calls=%async_computation.11 | async-start | bytes 13107200 | tf_op jit(solution)/shard_map/all_gather | solution.py:223
  266.3 10.2 %slice-start.4 = ((s8[7340032]{0:T(1024)(128)(4,1)}), s8[4194304]{0:T(1024)(128)(4,1)S(1)}, s32[]{:S(2)}) async-start(s8[7340032]{0:T(1024)(128)(4,1)} %bitcast.79), calls=%async_computation.16 | async-start | bytes 8388608
  266.6 9.9 %slice-start.5 = ((s8[7340032]{0:T(1024)(128)(4,1)}), s8[3145728]{0:T(1024)(128)(4,1)S(1)}, s32[]{:S(2)}) async-start(s8[7340032]{0:T(1024)(128)(4,1)} %bitcast.79), calls=%async_computation.17 | async-start | bytes 6291456
  379.6 1.7 copy-start.1
  381.3 1.1 copy-start.2
  385.0 31.7 %all-to-all-start.5 = ((bf16[8,4,16384]{2,1,0:T(4,128)(2,1)}), bf16[8,4,16384]{2,1,0:T(4,128)(2,1)S(1)}, u32[]{:S(2)}, u32[]{:S(2)}) async-start(bf16[8,4,16384]{2,1,0:T(4,128)(2,1)} %reshape.491), calls=%async_computation.7 | async-start | bytes 2097152 | tf_op jit(solution)/shard_map/all_to_all | solution.py:237
Sparse Core Ops, SparseCore 0:
  65.0 24.3 all-gather.3
  113.9 19.5 reduce-scatter.2
  190.0 58.8 reduce-scatter.4
  304.7 67.5 all-gather.5
